TPU v7x, 32 devices: a whole 2x2x4 slice. The times are simulated.
32 devices in a mesh: tok: 8 (over z, x), exp: 4 (over y, core).
Axes of the slice: x: 2, y: 2, z: 4, core: 2. Of those that a mesh axis runs over, the one named last changes fastest.
Arguments:
- tokens: bfloat16 [16384, 7168], P('tok', 'exp'), may hold values from -6 to 6
- gate_weight: bfloat16 [7168, 256], P('exp'), may hold values from -0.0625 to 0.0625
- expert_ids: int32 [16384, 8], P('tok'), may hold values from 0 to 255, all different within a row
- expert_bias: float32 [256], P('exp'), may hold values from -0.002 to 0.002
Outputs:
- affinities: float32 [16384, 256], P('tok', 'exp')
- weights: float32 [16384, 8], P('tok')
- load: float32 [256], replicated
- new_bias: float32 [256], replicated
All inputs are finite; a program needn't handle non-finite values.
Results may differ from a plain program's by a relative error of at most 0.0003.
Values may be sent and summed in bfloat16 or wider, within the bound.
A program may use at most 64 MiB of HBM per device.

v0:
```python
import jax
import jax.numpy as jnp
from jax import lax
from jax.sharding import PartitionSpec as P


def count_experts(expert_ids, width):
    numbers = lax.iota(jnp.int32, width)
    matches = expert_ids[:, :, None] == numbers[None, None, :]
    return jnp.sum(matches.astype(jnp.float32), axis=(0, 1))


def local(tokens, gate_weight, expert_ids, expert_bias):
    experts_all = gate_weight.shape[1]
    own_width = expert_bias.shape[0]
    first_expert = lax.axis_index("exp") * own_width
    tok_rows = tokens.shape[0]
    partial_logits = jnp.dot(tokens, gate_weight, preferred_element_type=jnp.float32)
    logits = lax.psum_scatter(partial_logits, "exp", scatter_dimension=1, tiled=True)
    affinities = jax.nn.sigmoid(logits)
    numbers = first_expert + lax.iota(jnp.int32, own_width)
    matches = expert_ids[:, :, None] == numbers[None, None, :]
    chosen_part = jnp.sum(jnp.where(matches, affinities[:, None, :], jnp.float32(0.0)), axis=2)
    chosen = lax.psum(chosen_part, "exp")
    weights = 2.5 * chosen / jnp.sum(chosen, axis=1, keepdims=True)
    target = jnp.float32(tok_rows * lax.axis_size("tok") * expert_ids.shape[1])
    bias_whole = lax.all_gather(expert_bias, "exp", axis=0, tiled=True)
    load = lax.psum(count_experts(expert_ids, experts_all), "tok")
    new_bias = bias_whole + 0.001 * jnp.sign(target - jnp.float32(experts_all) * load)
    return (affinities, weights, load, new_bias)


def solution(mesh):
    in_specs = (P("tok", "exp"), P("exp", None), P("tok", None), P("exp"))
    out_specs = (P("tok", "exp"), P("tok", None), P(), P())
    return jax.shard_map(local, mesh=mesh, in_specs=in_specs, out_specs=out_specs, check_vma=False)
```

profile of v0, /device:TPU:0, one launch (start us, length us, event | category | flops | bytes accessed | tf_op | source)
XLA Modules:
  0.0 92.7 jit_solution(2102868022089184914)
XLA Ops:
  7.2 0.0 copy-start
  7.2 0.0 copy-start.5
  7.2 0.0 reduce-scatter.2.cloned.1.call-start
  7.3 1.1 %copy-done = bf16[1792,256]{1,0:T(8,128)(2,1)S(1)} copy-done((bf16[1792,256]{1,0:T(8,128)(2,1)S(1)}, bf16[1792,256]{1,0:T(8,128)(2,1)}, u32[]{:S(2)}) %copy-start) | copy-done | bytes 917528
  8.4 6.5 %fusion = f32[2048,256]{0,1:T(8,128)} fusion(bf16[2048,1792]{1,0:T(8,128)(2,1)} %param.4, bf16[1792,256]{1,0:T(8,128)(2,1)S(1)} %copy-done), kind=kOutput, calls=%fused_computation.7 | convolution fusion | flops 1879048192 | bytes 10354688 | tf_op jit(solution)/shard_map/dot_general | solution.py:18
  14.9 0.0 reduce-scatter.2.cloned.1.call-update
  14.9 0.0 all-reduce.3.cloned.1.call-start
  15.0 0.3 copy.11
  15.4 0.6 dynamic-slice
  16.6 0.0 copy-done.4
  16.6 0.2 dynamic-update-slice
  16.9 5.1 %convert_reduce_fusion = f32[256]{0:T(256)S(1)} fusion(s32[2048,8]{1,0:T(8,128)S(1)} %copy.11), kind=kLoop, calls=%fused_computation | loop fusion | flops 12582656 | bytes 66560 | tf_op jit(solution)/shard_map/reduce_sum | solution.py:10
  22.0 23.1 %psum.15 = f32[256]{0:T(256)S(1)} all-reduce(f32[256]{0:T(256)S(1)} %convert_reduce_fusion), channel_id=1, replica_groups=mesh['tok'=8,'exp'=4] {'tok'}, use_global_device_ids=true, to_apply=%region_5.6 | all-reduce | flops 256 | bytes 2048 | tf_op jit(solution)/shard_map/psum | solution.py:28
  45.1 5.7 %all-reduce = f32[256]{0:T(256)S(1)} all-reduce(f32[256]{0:T(256)S(1)} %dynamic-update-slice), channel_id=1, replica_groups=mesh['tok'=8,'exp'=4] {'exp'}, use_global_device_ids=true, to_apply=%add | all-reduce | flops 256 | bytes 2048
  50.8 0.0 reduce-scatter.2.cloned.1.call-done
  50.8 1.2 %add_divide_fusion = f32[2048,64]{0,1:T(8,128)S(1)} fusion(f32[2048,64]{0,1:T(8,128)} %reduce-scatter.2.cloned.1.call-done), kind=kLoop, calls=%fused_computation.3 | loop fusion | flops 393216 | bytes 1048576 | tf_op jit(solution)/shard_map/div | solution.py:20
  52.0 0.0 copy-start.1
  52.0 1.2 %select_reduce_fusion = f32[2048,8]{0,1:T(8,128)} fusion(f32[2048,64]{0,1:T(8,128)S(1)} %add_divide_fusion, s32[2048,8]{0,1:T(8,128)S(1)} %copy-done.2, s32[64]{0:T(128)S(1)} %iota_add_fusion), kind=kLoop, calls=%fused_computation.2 | loop fusion | flops 3129344 | bytes 655616 | tf_op jit(solution)/shard_map/reduce_sum | solution.py:23
  53.2 0.0 all-reduce.3.cloned.1.call-update
  53.2 0.6 multiply_add_fusion
  53.8 29.7 %all-reduce.3.cloned.1.call-done = f32[2048,8]{0,1:T(8,128)} async-done(((f32[2048,8]{0,1:T(8,128)}), f32[2048,8]{0,1:T(8,128)}) %all-reduce.3.cloned.1.call-update) | async-done | bytes 65552 | tf_op jit(solution)/shard_map/psum | solution.py:24
  83.5 0.9 reduce_sum.28
  84.4 1.5 %multiply_divide_fusion = f32[2048,8]{0,1:T(8,128)} fusion(f32[2048,8]{0,1:T(8,128)} %all-reduce.3.cloned.1.call-done, f32[2048]{0:T(1024)S(1)} %reduce_sum.28), kind=kLoop, calls=%fused_computation.4 | loop fusion | flops 32768 | bytes 139264 | tf_op jit(solution)/shard_map/div | solution.py:25
  85.9 0.0 copy-done.3
  (8 shorter events, 0.0 us)
Async XLA Ops:
  7.2 1.2 %copy-start = (bf16[1792,256]{1,0:T(8,128)(2,1)S(1)}, bf16[1792,256]{1,0:T(8,128)(2,1)}, u32[]{:S(2)}) copy-start(bf16[1792,256]{1,0:T(8,128)(2,1)} %param.5) | copy-start | bytes 2752516
  7.2 8.2 %copy-start.5 = (u32[32]{0:T(128)S(1)}, u32[32]{0:T(128)}, u32[]{:S(2)}) copy-start(u32[32]{0:T(128)} %constant.20) | copy-start | bytes 388
  7.2 7.8 %copy-start.2 = (s32[2048,8]{0,1:T(8,128)S(1)}, s32[2048,8]{0,1:T(8,128)}, u32[]{:S(2)}) copy-start(s32[2048,8]{0,1:T(8,128)} %param.6) | copy-start | bytes 196612
  7.2 9.4 %copy-start.4 = (f32[64]{0:T(128)S(1)}, f32[64]{0:T(128)}, u32[]{:S(2)}) copy-start(f32[64]{0:T(128)} %param.7) | copy-start | bytes 772
  7.2 43.6 %reduce-scatter.2.cloned.1.call-start = ((), (), s32[]{:S(2)}) async-start(), calls=%async_computation.1 | async-start | bytes 2621440 | tf_op jit(solution)/shard_map/reduce_scatter | solution.py:19
  14.9 68.6 %all-reduce.3.cloned.1.call-start = ((), (), s32[]{:S(2)}) async-start(), calls=%async_computation.2 | async-start | bytes 131072 | tf_op jit(solution)/shard_map/psum | solution.py:24
  45.1 40.8 %copy-start.3 = (f32[256]{0:T(256)}, f32[256]{0:T(256)S(1)}, u32[]{:S(2)}) copy-start(f32[256]{0:T(256)S(1)} %psum.15) | copy-start | bytes 3076
  52.0 33.9 %copy-start.1 = (f32[2048,64]{0,1:T(8,128)}, f32[2048,64]{0,1:T(8,128)S(1)}, u32[]{:S(2)}) copy-start(f32[2048,64]{0,1:T(8,128)S(1)} %add_divide_fusion) | copy-start | bytes 1572868
Sparse Core Ops, SparseCore 0:
  15.1 33.8 reduce-scatter.1
  53.3 30.1 all-reduce.2
where the time goes:
time: 93.1 us; the launch traced here: 92.7 us
  waiting for transfers between devices  29.8 us (32%)
  blocking collectives  28.8 us (31%)
  between operations  14.8 us (16%)
  other arithmetic  10.4 us (11%)
  matrix products  6.53 us (7%)
  local copies, waits for them, and re-layouts  2.31 us (2%)
    psum x1, waiting for transfers between devices, local(): chosen = lax.psum(chosen_part, 'exp')  29.7 us
    psum x1, blocking collectives, local(): load = lax.psum(count_experts(expert_ids, experts_all), 'tok')  23.1 us
    dot_general x1, matrix products, local(): jnp.dot(tokens, gate_weight, preferred_element_type=jnp.float32)  6.53 us
    unnamed x1, blocking collectives  5.66 us
    reduce_sum x1, other arithmetic, count_experts(): return jnp.sum(matches.astype(jnp.float32), axis=(0, 1))  5.11 us
    unnamed x16, local copies, waits for them, and re-layouts  2.31 us
  transfers between devices with their start and end apart: 2, of which 1 were waited for; matrix products, arithmetic and copies ran while one was open for 7% of the time, Pallas kernels for 0%

commit v1 on v0

v1 whole, which is shorter than its diff:
```python
import functools

import jax
import jax.numpy as jnp
from jax import lax
from jax.experimental import pallas as pl
from jax.experimental.pallas import tpu as pltpu
from jax.sharding import PartitionSpec as P

MESH = pl.DeviceIdType.MESH
F32 = jnp.float32
LINK = jnp.int16
TOP_CODE = 32760.0
TOKEN_BOUND, GATE_BOUND = 6.0, 0.0625


def kernel(ntok, widths, x_hbm, w_hbm, ids_hbm, bias_hbm,
           aff_hbm, wts_hbm, load_ref, newb_ref,
           xv, wv, wt, ids, bias_own, bias_all, part, rx1, keep, tx2, rx2, mine, lin, lrx,
           affv, wtsv, cnt,
           x_sem, w_sem, i_sem, b_sem, s1, r1, s2, r2, s4, r4, sc, rc, sb, rb, ao, wo):
    own = bias_own.shape[1]
    n = len(widths)
    starts = [sum(widths[:i]) for i in range(n)]
    t, e = lax.axis_index("tok"), lax.axis_index("exp")
    y, c = e // 2, e % 2
    mate = 2 * y + 1 - c
    peer = 2 * (1 - y) + c
    cross = 2 * (1 - y) + 1 - c
    experts = 4 * own

    def cols(i):
        return pl.ds(starts[i], widths[i])

    ids_in = pltpu.make_async_copy(ids_hbm, ids, i_sem)
    b_in = pltpu.make_async_copy(bias_hbm, bias_own, b_sem)
    w_in = pltpu.make_async_copy(w_hbm, wv, w_sem)
    x_in = [pltpu.make_async_copy(x_hbm.at[cols(i)], xv.at[cols(i)], x_sem.at[i]) for i in range(n)]
    ids_in.start()
    b_in.start()
    w_in.start()
    for copy in x_in:
        copy.start()

    barrier = pltpu.get_barrier_semaphore()
    for other in (mate, peer, cross):
        pl.semaphore_signal(barrier, inc=1, device_id=(t, other), device_id_type=MESH)
    for d in range(1, ntok):
        pl.semaphore_signal(barrier, inc=1, device_id=((t + d) % ntok, e), device_id_type=MESH)

    w_in.wait()
    wt[...] = wv[...].T
    ids_in.wait()
    numbers = lax.broadcasted_iota(jnp.int32, (experts, 1), 0)
    lanes = 128
    acc = jnp.zeros((experts, lanes), F32)
    for g in range(ids.shape[1] // lanes):
        for j in range(ids.shape[0]):
            acc = acc + jnp.where(ids[j:j + 1, g * lanes:(g + 1) * lanes] == numbers, F32(1), F32(0))
    counts = lax.dot_general(jnp.ones((8, lanes), jnp.bfloat16), acc.astype(jnp.bfloat16),
                             (((1,), (1,)), ((), ())), preferred_element_type=F32)
    cnt[0] = counts.astype(jnp.int32)
    b_in.wait()
    bias_all[0] = jnp.broadcast_to(bias_own[...], bias_all.shape[1:])

    pl.semaphore_wait(barrier, 3 + ntok - 1)

    cnt_out = [pltpu.make_async_remote_copy(
        src_ref=cnt.at[0], dst_ref=cnt.at[d], send_sem=sc.at[d], recv_sem=rc.at[d],
        device_id=((t + d) % ntok, e), device_id_type=MESH) for d in range(1, ntok)]
    bias_out = [pltpu.make_async_remote_copy(
        src_ref=bias_own, dst_ref=bias_all.at[k, pl.ds(0, 1)], send_sem=sb.at[k], recv_sem=rb.at[k],
        device_id=(t, other), device_id_type=MESH) for k, other in ((1, mate), (2, peer), (3, cross))]
    for copy in cnt_out + bias_out:
        copy.start()

    def first(i):
        return pltpu.make_async_remote_copy(
            src_ref=part.at[:, 1 - c, :, cols(i)], dst_ref=rx1.at[:, :, cols(i)],
            send_sem=s1.at[i], recv_sem=r1.at[i], device_id=(t, mate), device_id_type=MESH)

    def second(i):
        return pltpu.make_async_remote_copy(
            src_ref=tx2.at[:, cols(i)], dst_ref=rx2.at[:, cols(i)],
            send_sem=s2.at[i], recv_sem=r2.at[i], device_id=(t, peer), device_id_type=MESH)

    def fourth(i):
        return pltpu.make_async_remote_copy(
            src_ref=lin.at[:, cols(i)], dst_ref=lrx.at[:, cols(i)],
            send_sem=s4.at[i], recv_sem=r4.at[i], device_id=(t, mate), device_id_type=MESH)

    local = lax.broadcasted_iota(jnp.int32, (own, 1), 0)

    def pick(i, values, block):
        rows = []
        base = local + block * own
        for j in range(ids.shape[0]):
            hit = ids[j:j + 1, cols(i)] == base
            rows.append(jnp.sum(jnp.where(hit, values, F32(0)), axis=0, keepdims=True))
        return jnp.concatenate(rows, axis=0)

    def stage_a(i):
        x_in[i].wait()
        r = lax.dot_general(wt[...], xv[cols(i)], (((1,), (1,)), ((), ())), preferred_element_type=F32)
        part[:, :, :, cols(i)] = r.reshape(2, 2, own, widths[i])
        first(i).start()

    grain = float(int(30000 / (2 * xv.shape[1] * TOKEN_BOUND * GATE_BOUND)))

    def step_of(whole):
        return whole * F32(1.0 / (grain * TOP_CODE))

    def stage_b(i):
        first(i).wait_recv()
        give = part[1 - y, c, :, cols(i)] + rx1[1 - y, :, cols(i)]
        held = part[y, c, :, cols(i)] + rx1[y, :, cols(i)]
        keep[:, cols(i)] = held
        largest = jnp.max(jnp.maximum(jnp.abs(give), jnp.abs(held)), axis=0, keepdims=True)
        whole = jnp.floor(largest * grain) + 1.0
        inverse = F32(grain * TOP_CODE) / whole
        code = jnp.round(give * inverse)
        chosen = jnp.round(pick(i, held, e) * inverse)
        tail = jnp.concatenate([chosen, jnp.broadcast_to(whole, chosen.shape)], axis=0)
        tx2[0:own, cols(i)] = code.astype(jnp.int32).astype(LINK)
        tx2[own:, cols(i)] = tail.astype(jnp.int32).astype(LINK)
        second(i).start()
        lin[:, cols(i)] = pick(i, code, peer) * step_of(whole)
        mine[:, cols(i)] = chosen * step_of(whole)

    out = {}

    def stage_c(i):
        second(i).wait_recv()
        code = rx2[0:own, cols(i)].astype(jnp.int32).astype(F32)
        tail = rx2[own:, cols(i)].astype(jnp.int32).astype(F32)
        top = ids.shape[0]
        step = step_of(tail[top:top + 1])
        logits = keep[:, cols(i)] + code * step
        ours = mine[:, cols(i)] + pick(i, code, e) * step
        theirs = lin[:, cols(i)] + tail[0:top] * step
        lin[:, cols(i)] = ours + theirs
        fourth(i).start()
        affv[:, cols(i)] = 1.0 / (1.0 + jnp.exp(-logits))
        out[i] = pltpu.make_async_copy(affv.at[:, cols(i)], aff_hbm.at[:, cols(i)], ao.at[i])
        out[i].start()

    def stage_d(i):
        fourth(i).wait_recv()
        chosen = 1.0 / (1.0 + jnp.exp(-(lin[:, cols(i)] + lrx[:, cols(i)])))
        wtsv[:, cols(i)] = 2.5 * chosen / jnp.sum(chosen, axis=0, keepdims=True)

    for step in range(n + 3):
        if step < n:
            stage_a(step)
        if 0 <= step - 1 < n:
            stage_b(step - 1)
        if step == n:
            for copy in cnt_out + bias_out:
                copy.wait()
            total = cnt[0]
            for d in range(1, ntok):
                total = total + cnt[d]
            load = total[0:1].astype(F32)
            load_ref[...] = load
            target = F32(ntok * ids.shape[1] * ids.shape[0])
            gap = target - F32(experts) * load
            sign = jnp.where(gap > 0, F32(1), jnp.where(gap < 0, F32(-1), F32(0)))
            b0, b1, b2, b3 = (bias_all[k, 0:1] for k in range(4))
            even = jnp.where(c == 0, b0, b1), jnp.where(c == 0, b1, b0)
            odd = jnp.where(c == 0, b2, b3), jnp.where(c == 0, b3, b2)
            low = [jnp.where(y == 0, p, q) for p, q in zip(even, odd)]
            high = [jnp.where(y == 0, q, p) for p, q in zip(even, odd)]
            bias = jnp.concatenate(low + high, axis=1)
            newb_ref[...] = bias + 0.001 * sign
        if 0 <= step - 3 < n:
            stage_c(step - 3)
        if 0 <= step - 4 < n:
            stage_d(step - 4)
    stage_d(n - 1)
    w_out = pltpu.make_async_copy(wtsv, wts_hbm, wo)
    w_out.start()
    for i in range(n):
        first(i).wait_send()
        second(i).wait_send()
        fourth(i).wait_send()
        out[i].wait()
    w_out.wait()


def local(ntok, tokens, gate_weight, expert_ids, expert_bias):
    rows, depth = tokens.shape
    experts = gate_weight.shape[1]
    own = expert_bias.shape[0]
    top = expert_ids.shape[1]
    piece = 256
    widths = [piece] * (rows // piece)
    n = len(widths)
    dma = pltpu.SemaphoreType.DMA
    vm = pltpu.VMEM
    any_ = pl.BlockSpec(memory_space=pl.ANY)
    vmem = pl.BlockSpec(memory_space=pltpu.VMEM)
    aff, wts, load, newb = pl.pallas_call(
        functools.partial(kernel, ntok, widths),
        out_shape=(
            jax.ShapeDtypeStruct((own, rows), F32),
            jax.ShapeDtypeStruct((top, rows), F32),
            jax.ShapeDtypeStruct((1, experts), F32),
            jax.ShapeDtypeStruct((1, experts), F32),
        ),
        in_specs=[any_] * 4,
        out_specs=(any_, any_, vmem, vmem),
        scratch_shapes=[
            vm((rows, depth), tokens.dtype), vm((depth, experts), gate_weight.dtype),
            vm((experts, depth), gate_weight.dtype), vm((top, rows), jnp.int32),
            vm((1, own), F32), vm((4, 8, own), F32),
            vm((2, 2, own, rows), F32), vm((2, own, rows), F32), vm((own, rows), F32),
            vm((own + 2 * top, rows), LINK), vm((own + 2 * top, rows), LINK),
            vm((top, rows), F32), vm((top, rows), F32), vm((top, rows), F32),
            vm((own, rows), F32), vm((top, rows), F32), vm((ntok, 8, experts), jnp.int32),
            dma((n,)), dma, dma, dma, dma((n,)), dma((n,)), dma((n,)), dma((n,)),
            dma((n,)), dma((n,)), dma((ntok,)), dma((ntok,)), dma((4,)), dma((4,)), dma((n,)), dma,
        ],
        compiler_params=pltpu.CompilerParams(
            collective_id=0, has_side_effects=True, vmem_limit_bytes=60 * 1024 * 1024),
    )(tokens, gate_weight, expert_ids.T, expert_bias.reshape(1, own))
    return aff.T, wts.T, load.reshape(experts), newb.reshape(experts)


def solution(mesh):
    in_specs = (P("tok", "exp"), P("exp", None), P("tok", None), P("exp"))
    out_specs = (P("tok", "exp"), P("tok", None), P(), P())
    return jax.shard_map(functools.partial(local, mesh.shape["tok"]), mesh=mesh,
                         in_specs=in_specs, out_specs=out_specs, check_vma=False)
```

time: 93.1 us -> 31.3 us (0.34)
  waiting for transfers between devices: 29.8 us -> 0 us
  blocking collectives: 28.8 us -> 0 us
  Pallas kernels: 0 us -> 24.7 us
  between operations: 14.8 us -> 0.64 us
  other arithmetic: 10.4 us -> 0 us
  matrix products: 6.53 us -> 0 us
  local copies, waits for them, and re-layouts: 2.31 us -> 5.79 us
    psum x1 -> x0, waiting for transfers between devices: 29.7 us -> none  [local(): chosen = lax.psum(chosen_part, 'exp')]
    pallas_call x0 -> x1, Pallas kernels: none -> 24.7 us  [local(): pl.pallas_call(functools.partial(kernel, ntok, widths), out_shape=(jax.Sh...]
    psum x1 -> x0, blocking collectives: 23.1 us -> none  [local(): load = lax.psum(count_experts(expert_ids, experts_all), 'tok')]
    reduce_sum x3 -> x0, other arithmetic: 7.17 us -> none  [the longest x1 5.11 us: count_experts(): return jnp.sum(matches.astype(jnp.float32), axis=(0, 1))]
    dot_general x1 -> x0, matrix products: 6.53 us -> none  [local(): jnp.dot(tokens, gate_weight, preferred_element_type=jnp.float32)]
    unnamed x1 -> x0, blocking collectives: 5.66 us -> none
    unnamed x16 -> x4, local copies, waits for them, and re-layouts: 2.31 us -> 5.79 us
    div x2 -> x0, other arithmetic: 2.67 us -> none  [the longest x1 1.49 us: local(): weights = 2.5 * chosen / jnp.sum(chosen, axis=1, keepdims=True)]
  transfers between devices with their start and end apart: 2 -> 0, of which waited for: 1 -> 0; matrix products, arithmetic and copies ran while one was open for 7% -> 0% of each run, Pallas kernels for 0% -> 0%
where the time goes in v1:
time: 31.3 us; the launch traced here: 31.1 us
  Pallas kernels  24.7 us (79%)
  local copies, waits for them, and re-layouts  5.79 us (18%)
  between operations  0.64 us (2%)
    pallas_call x1, Pallas kernels, local(): pl.pallas_call(functools.partial(kernel, ntok, widths), out_shape=(jax.Sh...  24.7 us
    unnamed x4, local copies, waits for them, and re-layouts  5.79 us

profile of v1, /device:TPU:0, one launch (start us, length us, event | category | flops | bytes accessed | tf_op | source)
XLA Modules:
  0.0 31.1 jit_solution(13573415625975042144)
XLA Ops:
  0.6 24.7 %shard_map.75 = (f32[64,2048]{1,0:T(8,128)}, f32[8,2048]{1,0:T(8,128)}, f32[1,256]{1,0:T(1,128)}, f32[1,256]{1,0:T(1,128)}) custom-call(bf16[2048,1792]{1,0:T(8,128)(2,1)} %x_hbm.1, bf16[1792,256]{1,0:T(8,128)(2,1)} %w_hbm.1, s32[8,2048]{1,0:T(8,128)} %bitcast.7, f32[1,64]{1,0:T(1,128)} %bitcast.11), custom_call_target="tpu_custom_call" | custom-call | tf_op jit(solution)/shard_map/pallas_call | solution.py:202
  25.3 1.9 %copy.12 = f32[2048,64]{0,1:T(8,128)} copy(f32[2048,64]{0,1:T(8,128)} %bitcast.6) | data formatting | bytes 1048576
  27.2 1.5 %copy.13 = f32[2048,8]{0,1:T(8,128)} copy(f32[2048,8]{0,1:T(8,128)} %bitcast.8) | data formatting | bytes 131072
  28.7 1.2 %copy.14 = f32[256]{0:T(256)} copy(f32[256]{0:T(256)} %bitcast.10) | data formatting | bytes 2048
  29.9 1.2 %copy.15 = f32[256]{0:T(256)} copy(f32[256]{0:T(256)} %bitcast.9) | data formatting | bytes 2048

commit v2 on v1

--- a/solution.py
+++ b/solution.py
@@ -15,10 +15,10 @@
 
 
 def kernel(ntok, widths, x_hbm, w_hbm, ids_hbm, bias_hbm,
-           aff_hbm, wts_hbm, load_ref, newb_ref,
+           affv, wtsv, load_ref, newb_ref,
            xv, wv, wt, ids, bias_own, bias_all, part, rx1, keep, tx2, rx2, mine, lin, lrx,
-           affv, wtsv, cnt,
-           x_sem, w_sem, i_sem, b_sem, s1, r1, s2, r2, s4, r4, sc, rc, sb, rb, ao, wo):
+           cnt_a, cnt,
+           x_sem, w_sem, i_sem, b_sem, s1, r1, s2, r2, s4, r4, sa, ra, sc, rc, sb, rb):
     own = bias_own.shape[1]
     n = len(widths)
     starts = [sum(widths[:i]) for i in range(n)]
@@ -36,10 +36,11 @@
     b_in = pltpu.make_async_copy(bias_hbm, bias_own, b_sem)
     w_in = pltpu.make_async_copy(w_hbm, wv, w_sem)
     x_in = [pltpu.make_async_copy(x_hbm.at[cols(i)], xv.at[cols(i)], x_sem.at[i]) for i in range(n)]
+    w_in.start()
     ids_in.start()
     b_in.start()
-    w_in.start()
-    for copy in x_in:
+    ahead = 2
+    for copy in x_in[:ahead]:
         copy.start()
 
     barrier = pltpu.get_barrier_semaphore()
@@ -48,30 +49,40 @@
     for d in range(1, ntok):
         pl.semaphore_signal(barrier, inc=1, device_id=((t + d) % ntok, e), device_id_type=MESH)
 
-    w_in.wait()
-    wt[...] = wv[...].T
     ids_in.wait()
-    numbers = lax.broadcasted_iota(jnp.int32, (experts, 1), 0)
     lanes = 128
-    acc = jnp.zeros((experts, lanes), F32)
-    for g in range(ids.shape[1] // lanes):
+    share = ids.shape[1] // 4
+    numbers = lax.broadcasted_iota(jnp.int32, (experts, lanes), 0).astype(F32).astype(jnp.bfloat16)
+    one, zero = jnp.bfloat16(1), jnp.bfloat16(0)
+    acc = jnp.zeros((experts, lanes), jnp.bfloat16)
+    for g in range(share // lanes):
+        at = pl.multiple_of(e * share + g * lanes, lanes)
+        found = ids[:, pl.ds(at, lanes)].astype(F32).astype(jnp.bfloat16)
         for j in range(ids.shape[0]):
-            acc = acc + jnp.where(ids[j:j + 1, g * lanes:(g + 1) * lanes] == numbers, F32(1), F32(0))
-    counts = lax.dot_general(jnp.ones((8, lanes), jnp.bfloat16), acc.astype(jnp.bfloat16),
+            acc = acc + jnp.where(found[j:j + 1] == numbers, one, zero)
+    counts = lax.dot_general(jnp.ones((8, lanes), jnp.bfloat16), acc,
                              (((1,), (1,)), ((), ())), preferred_element_type=F32)
-    cnt[0] = counts.astype(jnp.int32)
+    cnt_a[0] = counts.astype(jnp.int32)
     b_in.wait()
     bias_all[0] = jnp.broadcast_to(bias_own[...], bias_all.shape[1:])
+    w_in.wait()
+    for copy in x_in[ahead:2 * ahead]:
+        copy.start()
+    wt[...] = wv[...].T
 
     pl.semaphore_wait(barrier, 3 + ntok - 1)
 
+    group = ((1, mate), (2, peer), (3, cross))
+    share_out = [pltpu.make_async_remote_copy(
+        src_ref=cnt_a.at[0], dst_ref=cnt_a.at[k], send_sem=sa.at[k], recv_sem=ra.at[k],
+        device_id=(t, other), device_id_type=MESH) for k, other in group]
+    bias_out = [pltpu.make_async_remote_copy(
+        src_ref=bias_own, dst_ref=bias_all.at[k, pl.ds(0, 1)], send_sem=sb.at[k], recv_sem=rb.at[k],
+        device_id=(t, other), device_id_type=MESH) for k, other in group]
     cnt_out = [pltpu.make_async_remote_copy(
         src_ref=cnt.at[0], dst_ref=cnt.at[d], send_sem=sc.at[d], recv_sem=rc.at[d],
         device_id=((t + d) % ntok, e), device_id_type=MESH) for d in range(1, ntok)]
-    bias_out = [pltpu.make_async_remote_copy(
-        src_ref=bias_own, dst_ref=bias_all.at[k, pl.ds(0, 1)], send_sem=sb.at[k], recv_sem=rb.at[k],
-        device_id=(t, other), device_id_type=MESH) for k, other in ((1, mate), (2, peer), (3, cross))]
-    for copy in cnt_out + bias_out:
+    for copy in share_out + bias_out:
         copy.start()
 
     def first(i):
@@ -101,6 +112,8 @@
 
     def stage_a(i):
         x_in[i].wait()
+        if i + 2 * ahead < n:
+            x_in[i + 2 * ahead].start()
         r = lax.dot_general(wt[...], xv[cols(i)], (((1,), (1,)), ((), ())), preferred_element_type=F32)
         part[:, :, :, cols(i)] = r.reshape(2, 2, own, widths[i])
         first(i).start()
@@ -127,8 +140,6 @@
         lin[:, cols(i)] = pick(i, code, peer) * step_of(whole)
         mine[:, cols(i)] = chosen * step_of(whole)
 
-    out = {}
-
     def stage_c(i):
         second(i).wait_recv()
         code = rx2[0:own, cols(i)].astype(jnp.int32).astype(F32)
@@ -141,50 +152,56 @@
         lin[:, cols(i)] = ours + theirs
         fourth(i).start()
         affv[:, cols(i)] = 1.0 / (1.0 + jnp.exp(-logits))
-        out[i] = pltpu.make_async_copy(affv.at[:, cols(i)], aff_hbm.at[:, cols(i)], ao.at[i])
-        out[i].start()
 
     def stage_d(i):
         fourth(i).wait_recv()
         chosen = 1.0 / (1.0 + jnp.exp(-(lin[:, cols(i)] + lrx[:, cols(i)])))
         wtsv[:, cols(i)] = 2.5 * chosen / jnp.sum(chosen, axis=0, keepdims=True)
 
-    for step in range(n + 3):
+    def merge_counts():
+        for copy in share_out:
+            copy.wait()
+        cnt[0] = (cnt_a[0] + cnt_a[1]) + (cnt_a[2] + cnt_a[3])
+        for copy in cnt_out:
+            copy.start()
+
+    def finish_counts():
+        for copy in cnt_out + bias_out:
+            copy.wait()
+        total = cnt[0]
+        for d in range(1, ntok):
+            total = total + cnt[d]
+        load = total[0:1].astype(F32)
+        load_ref[...] = load
+        target = F32(ntok * ids.shape[1] * ids.shape[0])
+        gap = target - F32(experts) * load
+        sign = jnp.where(gap > 0, F32(1), jnp.where(gap < 0, F32(-1), F32(0)))
+        b0, b1, b2, b3 = (bias_all[k, 0:1] for k in range(4))
+        near = jnp.where(c == 0, b0, b1), jnp.where(c == 0, b1, b0)
+        far = jnp.where(c == 0, b2, b3), jnp.where(c == 0, b3, b2)
+        low = [jnp.where(y == 0, p, q) for p, q in zip(near, far)]
+        high = [jnp.where(y == 0, q, p) for p, q in zip(near, far)]
+        bias = jnp.concatenate(low + high, axis=1)
+        newb_ref[...] = bias + 0.001 * sign
+
+    lag_b, lag_c, lag_d = 2, 7, 8
+    for step in range(n + lag_d):
         if step < n:
             stage_a(step)
-        if 0 <= step - 1 < n:
-            stage_b(step - 1)
-        if step == n:
-            for copy in cnt_out + bias_out:
-                copy.wait()
-            total = cnt[0]
-            for d in range(1, ntok):
-                total = total + cnt[d]
-            load = total[0:1].astype(F32)
-            load_ref[...] = load
-            target = F32(ntok * ids.shape[1] * ids.shape[0])
-            gap = target - F32(experts) * load
-            sign = jnp.where(gap > 0, F32(1), jnp.where(gap < 0, F32(-1), F32(0)))
-            b0, b1, b2, b3 = (bias_all[k, 0:1] for k in range(4))
-            even = jnp.where(c == 0, b0, b1), jnp.where(c == 0, b1, b0)
-            odd = jnp.where(c == 0, b2, b3), jnp.where(c == 0, b3, b2)
-            low = [jnp.where(y == 0, p, q) for p, q in zip(even, odd)]
-            high = [jnp.where(y == 0, q, p) for p, q in zip(even, odd)]
-            bias = jnp.concatenate(low + high, axis=1)
-            newb_ref[...] = bias + 0.001 * sign
-        if 0 <= step - 3 < n:
-            stage_c(step - 3)
-        if 0 <= step - 4 < n:
-            stage_d(step - 4)
-    stage_d(n - 1)
-    w_out = pltpu.make_async_copy(wtsv, wts_hbm, wo)
-    w_out.start()
+        if 0 <= step - lag_b < n:
+            stage_b(step - lag_b)
+        if step == n // 2:
+            merge_counts()
+        if step == n + lag_b:
+            finish_counts()
+        if 0 <= step - lag_c < n:
+            stage_c(step - lag_c)
+        if 0 <= step - lag_d < n:
+            stage_d(step - lag_d)
     for i in range(n):
         first(i).wait_send()
         second(i).wait_send()
         fourth(i).wait_send()
-        out[i].wait()
-    w_out.wait()
 
 
 def local(ntok, tokens, gate_weight, expert_ids, expert_bias):
@@ -199,16 +216,12 @@
     vm = pltpu.VMEM
     any_ = pl.BlockSpec(memory_space=pl.ANY)
     vmem = pl.BlockSpec(memory_space=pltpu.VMEM)
-    aff, wts, load, newb = pl.pallas_call(
+    shapes = ((own, rows), (top, rows), (1, experts), (1, experts))
+    results = pl.pallas_call(
         functools.partial(kernel, ntok, widths),
-        out_shape=(
-            jax.ShapeDtypeStruct((own, rows), F32),
-            jax.ShapeDtypeStruct((top, rows), F32),
-            jax.ShapeDtypeStruct((1, experts), F32),
-            jax.ShapeDtypeStruct((1, experts), F32),
-        ),
+        out_shape=tuple(pltpu.VMEM(shape, F32) for shape in shapes),
         in_specs=[any_] * 4,
-        out_specs=(any_, any_, vmem, vmem),
+        out_specs=(vmem,) * 4,
         scratch_shapes=[
             vm((rows, depth), tokens.dtype), vm((depth, experts), gate_weight.dtype),
             vm((experts, depth), gate_weight.dtype), vm((top, rows), jnp.int32),
@@ -216,13 +229,14 @@
             vm((2, 2, own, rows), F32), vm((2, own, rows), F32), vm((own, rows), F32),
             vm((own + 2 * top, rows), LINK), vm((own + 2 * top, rows), LINK),
             vm((top, rows), F32), vm((top, rows), F32), vm((top, rows), F32),
-            vm((own, rows), F32), vm((top, rows), F32), vm((ntok, 8, experts), jnp.int32),
+            vm((4, 8, experts), jnp.int32), vm((ntok, 8, experts), jnp.int32),
             dma((n,)), dma, dma, dma, dma((n,)), dma((n,)), dma((n,)), dma((n,)),
-            dma((n,)), dma((n,)), dma((ntok,)), dma((ntok,)), dma((4,)), dma((4,)), dma((n,)), dma,
+            dma((n,)), dma((n,)), dma((4,)), dma((4,)), dma((ntok,)), dma((ntok,)), dma((4,)), dma((4,)),
         ],
         compiler_params=pltpu.CompilerParams(
             collective_id=0, has_side_effects=True, vmem_limit_bytes=60 * 1024 * 1024),
     )(tokens, gate_weight, expert_ids.T, expert_bias.reshape(1, own))
+    aff, wts, load, newb = results
     return aff.T, wts.T, load.reshape(experts), newb.reshape(experts)
 
 

time: 31.3 us -> 22.9 us (0.73)
  Pallas kernels: 24.7 us -> 19.5 us
  local copies, waits for them, and re-layouts: 5.79 us -> 2.55 us
    pallas_call x1, Pallas kernels: 24.7 us -> 19.5 us  [local(): pl.pallas_call(functools.partial(kernel, ntok, widths), out_shape=tuple((...]
    unnamed x4, local copies, waits for them, and re-layouts: 5.79 us -> 2.55 us
where the time goes in v2:
time: 22.9 us; the launch traced here: 22.7 us
  Pallas kernels  19.5 us (85%)
  local copies, waits for them, and re-layouts  2.55 us (11%)
  between operations  0.64 us (3%)
    pallas_call x1, Pallas kernels, local(): pl.pallas_call(functools.partial(kernel, ntok, widths), out_shape=tuple((...  19.5 us
    unnamed x4, local copies, waits for them, and re-layouts  2.55 us

profile of v2, /device:TPU:0, one launch (start us, length us, event | category | flops | bytes accessed | tf_op | source)
XLA Modules:
  0.0 22.7 jit_solution(3507392194157441252)
XLA Ops:
  0.6 19.5 %shard_map.75 = (f32[64,2048]{1,0:T(8,128)S(1)}, f32[8,2048]{1,0:T(8,128)S(1)}, f32[1,256]{1,0:T(1,128)S(1)}, f32[1,256]{1,0:T(1,128)S(1)}) custom-call(bf16[2048,1792]{1,0:T(8,128)(2,1)} %x_hbm.1, bf16[1792,256]{1,0:T(8,128)(2,1)} %w_hbm.1, s32[8,2048]{1,0:T(8,128)} %bitcast.10, f32[1,64]{1,0:T(1,128)} %bitcast.11), custom_call_target="tpu_custom_call" | custom-call | tf_op jit(solution)/shard_map/pallas_call | solution.py:220
  20.2 0.8 %copy.12 = f32[2048,64]{0,1:T(8,128)} copy(f32[2048,64]{0,1:T(8,128)S(1)} %bitcast.6) | data formatting | bytes 1048576
  21.0 0.6 %copy.13 = f32[2048,8]{0,1:T(8,128)} copy(f32[2048,8]{0,1:T(8,128)S(1)} %bitcast.7) | data formatting | bytes 131072
  21.6 0.6 %copy.14 = f32[256]{0:T(256)} copy(f32[256]{0:T(256)S(1)} %bitcast.9) | data formatting | bytes 2048
  22.1 0.6 %copy.15 = f32[256]{0:T(256)} copy(f32[256]{0:T(256)S(1)} %bitcast.8) | data formatting | bytes 2048

commit v3 on v2

--- a/solution.py
+++ b/solution.py
@@ -204,13 +204,22 @@
         fourth(i).wait_send()
 
 
+def place(aff, wts, load, newb, aff_hbm, wts_hbm, load_hbm, newb_hbm, sem):
+    copies = [pltpu.make_async_copy(a, b, sem.at[k]) for k, (a, b) in enumerate(
+        ((aff, aff_hbm), (wts, wts_hbm), (load, load_hbm), (newb, newb_hbm)))]
+    for copy in copies:
+        copy.start()
+    for copy in copies:
+        copy.wait()
+
+
 def local(ntok, tokens, gate_weight, expert_ids, expert_bias):
     rows, depth = tokens.shape
     experts = gate_weight.shape[1]
     own = expert_bias.shape[0]
     top = expert_ids.shape[1]
     piece = 256
-    widths = [piece] * (rows // piece)
+    widths = [piece // 2] * 2 + [piece] * (rows // piece - 1)
     n = len(widths)
     dma = pltpu.SemaphoreType.DMA
     vm = pltpu.VMEM
@@ -236,7 +245,13 @@
         compiler_params=pltpu.CompilerParams(
             collective_id=0, has_side_effects=True, vmem_limit_bytes=60 * 1024 * 1024),
     )(tokens, gate_weight, expert_ids.T, expert_bias.reshape(1, own))
-    aff, wts, load, newb = results
+    aff, wts, load, newb = pl.pallas_call(
+        place,
+        out_shape=tuple(jax.ShapeDtypeStruct(shape, F32) for shape in shapes),
+        in_specs=[vmem] * 4,
+        out_specs=(pl.BlockSpec(memory_space=pltpu.HBM),) * 4,
+        scratch_shapes=[dma((4,))],
+    )(*(pltpu.with_memory_space_constraint(r, pltpu.VMEM) for r in results))
     return aff.T, wts.T, load.reshape(experts), newb.reshape(experts)
 
 

time: 22.9 us -> 21.6 us (0.943)
  local copies, waits for them, and re-layouts: 2.55 us -> 0 us
  Pallas kernels: 19.5 us -> 20.8 us
    unnamed x4 -> x0, local copies, waits for them, and re-layouts: 2.55 us -> none
    pallas_call x0 -> x1, Pallas kernels: none -> 0.84 us  [local(): pl.pallas_call(place, out_shape=tuple((jax.ShapeDtypeStruct(shape, F32) f...]
    pallas_call x1, Pallas kernels: 19.5 us -> 20 us  [local(): pl.pallas_call(functools.partial(kernel, ntok, widths), out_shape=tuple((...]
where the time goes in v3:
time: 21.6 us; the launch traced here: 21.5 us
  Pallas kernels  20.8 us (96%)
  between operations  0.64 us (3%)
    pallas_call x1, Pallas kernels, local(): pl.pallas_call(functools.partial(kernel, ntok, widths), out_shape=tuple((...  20 us
    pallas_call x1, Pallas kernels, local(): pl.pallas_call(place, out_shape=tuple((jax.ShapeDtypeStruct(shape, F32) f...  0.84 us

profile of v3, /device:TPU:0, one launch (start us, length us, event | category | flops | bytes accessed | tf_op | source)
XLA Modules:
  0.0 21.5 jit_solution(15237611040800737802)
XLA Ops:
  0.6 20.0 %shard_map.75 = (f32[64,2048]{1,0:T(8,128)S(1)}, f32[8,2048]{1,0:T(8,128)S(1)}, f32[1,256]{1,0:T(1,128)S(1)}, f32[1,256]{1,0:T(1,128)S(1)}) custom-call(bf16[2048,1792]{1,0:T(8,128)(2,1)} %x_hbm.1, bf16[1792,256]{1,0:T(8,128)(2,1)} %w_hbm.1, s32[8,2048]{1,0:T(8,128)} %bitcast.6, f32[1,64]{1,0:T(1,128)} %bitcast.7), custom_call_target="tpu_custom_call" | custom-call | tf_op jit(solution)/shard_map/pallas_call | solution.py:229
  20.6 0.8 %shard_map.76 = (f32[64,2048]{1,0:T(8,128)}, f32[8,2048]{1,0:T(8,128)}, f32[1,256]{1,0:T(1,128)}, f32[1,256]{1,0:T(1,128)}) custom-call(f32[64,2048]{1,0:T(8,128)S(1)} %get-tuple-element.12.aff, f32[8,2048]{1,0:T(8,128)S(1)} %get-tuple-element.13.wts, f32[1,256]{1,0:T(1,128)S(1)} %get-tuple-element.14.load, f32[1,256]{1,0:T(1,128)S(1)} %get-tuple-element.15.newb), custom_call_target="tpu_custom_call" | custom-call | tf_op jit(solution)/shard_map/pallas_call | solution.py:248

commit v4 on v3

--- a/solution.py
+++ b/solution.py
@@ -39,7 +39,7 @@
     w_in.start()
     ids_in.start()
     b_in.start()
-    ahead = 2
+    ahead = 3
     for copy in x_in[:ahead]:
         copy.start()
 
@@ -219,7 +219,7 @@
     own = expert_bias.shape[0]
     top = expert_ids.shape[1]
     piece = 256
-    widths = [piece // 2] * 2 + [piece] * (rows // piece - 1)
+    widths = [piece // 2] * 2 + [piece] * (rows // piece - 2) + [piece // 2] * 2
     n = len(widths)
     dma = pltpu.SemaphoreType.DMA
     vm = pltpu.VMEM

time: 21.6 us -> 22.4 us (1.037)
  Pallas kernels: 20.8 us -> 21.6 us
    pallas_call x1, Pallas kernels: 20 us -> 20.8 us  [local(): pl.pallas_call(functools.partial(kernel, ntok, widths), out_shape=tuple((...]
where the time goes in v4:
time: 22.4 us; the launch traced here: 22.3 us
  Pallas kernels  21.6 us (96%)
  between operations  0.64 us (3%)
    pallas_call x1, Pallas kernels, local(): pl.pallas_call(functools.partial(kernel, ntok, widths), out_shape=tuple((...  20.8 us
    pallas_call x1, Pallas kernels, local(): pl.pallas_call(place, out_shape=tuple((jax.ShapeDtypeStruct(shape, F32) f...  0.84 us

profile of v4, /device:TPU:0, one launch (start us, length us, event | category | flops | bytes accessed | tf_op | source)
XLA Modules:
  0.0 22.3 jit_solution(10829026572691860569)
XLA Ops:
  0.6 20.8 %shard_map.75 = (f32[64,2048]{1,0:T(8,128)S(1)}, f32[8,2048]{1,0:T(8,128)S(1)}, f32[1,256]{1,0:T(1,128)S(1)}, f32[1,256]{1,0:T(1,128)S(1)}) custom-call(bf16[2048,1792]{1,0:T(8,128)(2,1)} %x_hbm.1, bf16[1792,256]{1,0:T(8,128)(2,1)} %w_hbm.1, s32[8,2048]{1,0:T(8,128)} %bitcast.6, f32[1,64]{1,0:T(1,128)} %bitcast.7), custom_call_target="tpu_custom_call" | custom-call | tf_op jit(solution)/shard_map/pallas_call | solution.py:229
  21.4 0.8 %shard_map.76 = (f32[64,2048]{1,0:T(8,128)}, f32[8,2048]{1,0:T(8,128)}, f32[1,256]{1,0:T(1,128)}, f32[1,256]{1,0:T(1,128)}) custom-call(f32[64,2048]{1,0:T(8,128)S(1)} %get-tuple-element.12.aff, f32[8,2048]{1,0:T(8,128)S(1)} %get-tuple-element.13.wts, f32[1,256]{1,0:T(1,128)S(1)} %get-tuple-element.14.load, f32[1,256]{1,0:T(1,128)S(1)} %get-tuple-element.15.newb), custom_call_target="tpu_custom_call" | custom-call | tf_op jit(solution)/shard_map/pallas_call | solution.py:248

commit v5 on v3

--- a/solution.py
+++ b/solution.py
@@ -46,8 +46,10 @@
     barrier = pltpu.get_barrier_semaphore()
     for other in (mate, peer, cross):
         pl.semaphore_signal(barrier, inc=1, device_id=(t, other), device_id_type=MESH)
-    for d in range(1, ntok):
-        pl.semaphore_signal(barrier, inc=1, device_id=((t + d) % ntok, e), device_id_type=MESH)
+    bits = [1 << k for k in range(ntok.bit_length() - 1)]
+    pairs = [t + bit - 2 * bit * ((t // bit) % 2) for bit in bits]
+    for other in pairs:
+        pl.semaphore_signal(barrier, inc=1, device_id=(other, e), device_id_type=MESH)
 
     ids_in.wait()
     lanes = 128
@@ -70,7 +72,7 @@
         copy.start()
     wt[...] = wv[...].T
 
-    pl.semaphore_wait(barrier, 3 + ntok - 1)
+    pl.semaphore_wait(barrier, 3 + len(pairs))
 
     group = ((1, mate), (2, peer), (3, cross))
     share_out = [pltpu.make_async_remote_copy(
@@ -80,8 +82,8 @@
         src_ref=bias_own, dst_ref=bias_all.at[k, pl.ds(0, 1)], send_sem=sb.at[k], recv_sem=rb.at[k],
         device_id=(t, other), device_id_type=MESH) for k, other in group]
     cnt_out = [pltpu.make_async_remote_copy(
-        src_ref=cnt.at[0], dst_ref=cnt.at[d], send_sem=sc.at[d], recv_sem=rc.at[d],
-        device_id=((t + d) % ntok, e), device_id_type=MESH) for d in range(1, ntok)]
+        src_ref=cnt.at[2 * k], dst_ref=cnt.at[2 * k + 1], send_sem=sc.at[k], recv_sem=rc.at[k],
+        device_id=(other, e), device_id_type=MESH) for k, other in enumerate(pairs)]
     for copy in share_out + bias_out:
         copy.start()
 
@@ -162,15 +164,18 @@
         for copy in share_out:
             copy.wait()
         cnt[0] = (cnt_a[0] + cnt_a[1]) + (cnt_a[2] + cnt_a[3])
-        for copy in cnt_out:
-            copy.start()
+        cnt_out[0].start()
+
+    def double_counts(k):
+        cnt_out[k].wait()
+        cnt[2 * k + 2] = cnt[2 * k] + cnt[2 * k + 1]
+        if k + 1 < len(pairs):
+            cnt_out[k + 1].start()
 
     def finish_counts():
-        for copy in cnt_out + bias_out:
+        for copy in bias_out:
             copy.wait()
-        total = cnt[0]
-        for d in range(1, ntok):
-            total = total + cnt[d]
+        total = cnt[2 * len(pairs)]
         load = total[0:1].astype(F32)
         load_ref[...] = load
         target = F32(ntok * ids.shape[1] * ids.shape[0])
@@ -185,6 +190,7 @@
         newb_ref[...] = bias + 0.001 * sign
 
     lag_b, lag_c, lag_d = 2, 7, 8
+    spacing = (n + lag_d - 2 - n // 2) // len(pairs)
     for step in range(n + lag_d):
         if step < n:
             stage_a(step)
@@ -192,8 +198,11 @@
             stage_b(step - lag_b)
         if step == n // 2:
             merge_counts()
-        if step == n + lag_b:
-            finish_counts()
+        for k in range(len(pairs)):
+            if step == n // 2 + (k + 1) * spacing:
+                double_counts(k)
+                if k + 1 == len(pairs):
+                    finish_counts()
         if 0 <= step - lag_c < n:
             stage_c(step - lag_c)
         if 0 <= step - lag_d < n:

time: 21.6 us -> 22.1 us (1.023)
  Pallas kernels: 20.8 us -> 21.3 us
    pallas_call x1, Pallas kernels: 20 us -> 20.5 us  [local(): pl.pallas_call(functools.partial(kernel, ntok, widths), out_shape=tuple((...]
where the time goes in v5:
time: 22.1 us; the launch traced here: 21.9 us
  Pallas kernels  21.3 us (96%)
  between operations  0.64 us (3%)
    pallas_call x1, Pallas kernels, local(): pl.pallas_call(functools.partial(kernel, ntok, widths), out_shape=tuple((...  20.5 us
    pallas_call x1, Pallas kernels, local(): pl.pallas_call(place, out_shape=tuple((jax.ShapeDtypeStruct(shape, F32) f...  0.84 us

profile of v5, /device:TPU:0, one launch (start us, length us, event | category | flops | bytes accessed | tf_op | source)
XLA Modules:
  0.0 21.9 jit_solution(17764226558068735784)
XLA Ops:
  0.6 20.5 %shard_map.75 = (f32[64,2048]{1,0:T(8,128)S(1)}, f32[8,2048]{1,0:T(8,128)S(1)}, f32[1,256]{1,0:T(1,128)S(1)}, f32[1,256]{1,0:T(1,128)S(1)}) custom-call(bf16[2048,1792]{1,0:T(8,128)(2,1)} %x_hbm.1, bf16[1792,256]{1,0:T(8,128)(2,1)} %w_hbm.1, s32[8,2048]{1,0:T(8,128)} %bitcast.6, f32[1,64]{1,0:T(1,128)} %bitcast.7), custom_call_target="tpu_custom_call" | custom-call | tf_op jit(solution)/shard_map/pallas_call | solution.py:238
  21.1 0.8 %shard_map.76 = (f32[64,2048]{1,0:T(8,128)}, f32[8,2048]{1,0:T(8,128)}, f32[1,256]{1,0:T(1,128)}, f32[1,256]{1,0:T(1,128)}) custom-call(f32[64,2048]{1,0:T(8,128)S(1)} %get-tuple-element.12.aff, f32[8,2048]{1,0:T(8,128)S(1)} %get-tuple-element.13.wts, f32[1,256]{1,0:T(1,128)S(1)} %get-tuple-element.14.load, f32[1,256]{1,0:T(1,128)S(1)} %get-tuple-element.15.newb), custom_call_target="tpu_custom_call" | custom-call | tf_op jit(solution)/shard_map/pallas_call | solution.py:257
